TPU v7x, 256 devices: a 8x8x2 block of a 8x8x16 slice. The times are simulated.
256 devices in a mesh: groups: 2 (over z), ep: 128 (over y, x, core).
Axes of the slice: x: 8, y: 8, z: 2, core: 2. Of those that a mesh axis runs over, the one named last changes fastest.
The devices are a block of a 8x8x16 slice.
Arguments:
- tokens: bfloat16 [2048, 2880], P(('groups', 'ep')), parts along dimension 0, may hold values from -6 to 6
- norm_gain: float32 [2880], replicated, may hold values from 0.1 to 1.9
- expert_ids: int32 [2048, 4], P(('groups', 'ep')), parts along dimension 0, may hold values from 0 to 63, all different within a row; in each aligned block of 8 rows (0 to 7, 8 to 15, ...) at most 1 rows name the same one
- gate_codes: int32 [2048, 4], P(('groups', 'ep')), parts along dimension 0, may hold values from 1 to 65535
- w_gate: bfloat16 [128, 2880, 720], P('ep'), may hold values from -0.109375 to 0.109375
- w_up: bfloat16 [128, 2880, 720], P('ep'), may hold values from -0.109375 to 0.109375
- w_down: bfloat16 [128, 720, 2880], P('ep'), may hold values from -0.15625 to 0.15625
Outputs:
- updated: bfloat16 [2048, 2880], P(('groups', 'ep')), parts along dimension 0
There are 2 independent parts, one for each index of `groups`. A program takes and returns all parts, laid end to end along the dimension named above; an argument that names none is the same for every part. Nothing has to cross between parts.
Inputs may be any that keep to these rules, and one draw needn't show every extreme that they name: `expert_ids`: each token names 4 different experts. Among the tokens of one device (aligned blocks of 8 rows) no expert is named more than once, and in every draw some expert is named exactly once by some device's tokens.
All inputs are finite; a program needn't handle non-finite values.
Results may differ from a plain program's by a relative error of at most 0.0049.
Values may be sent and summed in bfloat16 or wider, within the bound.
A program may use at most 64 MiB of HBM per device.

v0:
```python
import jax
import jax.numpy as jnp
from jax import lax
from jax.sharding import PartitionSpec as P

epsilon = 1e-05


def from_partner(array, axis, bit):
    return lax.ppermute(array, axis, [(i, i ^ 1 << bit) for i in range(lax.axis_size(axis))])


def shards(tokens, norm_gain, expert_ids, gate_codes, w_gate, w_up, w_down):
    values = tokens.astype(jnp.float32)
    normed = (
        values * lax.rsqrt(jnp.mean(values * values, axis=1, keepdims=True) + epsilon) * norm_gain
    ).astype(jnp.bfloat16)
    code_values = gate_codes.astype(jnp.float32)
    weights = code_values / jnp.sum(code_values, axis=1, keepdims=True)
    token_count, top_count = expert_ids.shape
    model_width = tokens.shape[1]
    half_width = model_width // 2
    devices = lax.axis_size("ep")
    experts = devices // 2
    capacity = 2 * token_count * top_count // experts
    flat_ids = expert_ids.reshape(-1)
    onehot = (flat_ids[:, None] == jnp.arange(experts, dtype=jnp.int32)[None, :]).astype(jnp.int32)
    earlier = jnp.cumsum(onehot, axis=0) - onehot
    position = jnp.sum(earlier * onehot, axis=1)
    target = flat_ids * capacity + position
    placing = (target[None, :] == jnp.arange(experts * capacity, dtype=jnp.int32)[:, None]).astype(
        jnp.bfloat16
    )
    repeated = jnp.repeat(normed, top_count, axis=0)
    buffer = jnp.dot(placing, repeated, preferred_element_type=jnp.float32).astype(jnp.bfloat16)
    buffer = buffer.reshape(experts, capacity, model_width)
    parity = lax.axis_index("ep") % 2
    outgoing = buffer.reshape(experts, capacity, 2, half_width)
    outgoing = jnp.transpose(outgoing, (0, 2, 1, 3)).reshape(devices, capacity, half_width)
    arrived = lax.all_to_all(outgoing, "ep", split_axis=0, concat_axis=0, tiled=True)
    partner = from_partner(arrived, "ep", 0)
    lower_half = jnp.where(parity == 0, arrived, partner)
    upper_half = jnp.where(parity == 0, partner, arrived)
    arrived = jnp.concatenate([lower_half, upper_half], axis=2)
    sources = arrived.shape[0]
    slot_count = arrived.shape[1]
    token_rows = arrived.reshape(sources * slot_count, model_width)
    gate_out = jnp.dot(token_rows, w_gate[0], preferred_element_type=jnp.float32)
    upward = jnp.dot(token_rows, w_up[0], preferred_element_type=jnp.float32)
    hidden = (jax.nn.silu(gate_out) * upward).astype(jnp.bfloat16)
    partial_out = jnp.dot(hidden, w_down[0], preferred_element_type=jnp.float32).astype(
        jnp.bfloat16
    )
    partial_out = partial_out.reshape(sources, slot_count, model_width)
    blocks = partial_out.reshape(sources, slot_count, 2, half_width)
    own_block = jnp.where(parity == 0, blocks[:, :, 0], blocks[:, :, 1])
    sent_block = jnp.where(parity == 0, blocks[:, :, 1], blocks[:, :, 0])
    other_block = from_partner(sent_block, "ep", 0)
    summed = (own_block.astype(jnp.float32) + other_block.astype(jnp.float32)).astype(jnp.bfloat16)
    returned = lax.all_to_all(summed, "ep", split_axis=0, concat_axis=0, tiled=True)
    returned = returned.reshape(experts, 2, slot_count, half_width)
    results = jnp.transpose(returned, (0, 2, 1, 3)).reshape(experts, slot_count, model_width)
    per_pair = jnp.dot(
        placing.T,
        results.reshape(experts * capacity, model_width),
        preferred_element_type=jnp.float32,
    )
    mixture = jnp.sum(
        per_pair.reshape(token_count, top_count, model_width) * weights[:, :, None], axis=1
    )
    return (values + mixture).astype(jnp.bfloat16)


def solution(mesh):
    return jax.shard_map(
        shards,
        mesh=mesh,
        in_specs=(
            P(("groups", "ep"), None),
            P(),
            P(("groups", "ep"), None),
            P(("groups", "ep"), None),
            P("ep", None, None),
            P("ep", None, None),
            P("ep", None, None),
        ),
        out_specs=P(("groups", "ep"), None),
        check_vma=False,
    )
```

profile of v0, /device:TPU:513, one launch (start us, length us, event | category | flops | bytes accessed | tf_op | source)
XLA Modules:
  0.0 101.0 jit_solution(11099089923835672365)
XLA Ops:
  0.0 0.9 fusion.25
  0.9 0.8 copy.25
  1.7 0.1 reshape.97
  1.8 0.1 fusion.30
  1.9 0.1 reduce_window_sum.11
  1.9 0.2 select_reduce_fusion
  2.1 0.9 fusion.27
  3.0 0.1 broadcast_in_dim.2
  3.1 0.1 reshape.98
  3.1 0.2 convolution_convert_fusion
  3.4 0.6 reshape_transpose_reshape_reshape.4
  4.0 0.5 broadcast.64
  4.5 3.2 %reduce.1 = bf16[128,1440]{1,0:T(8,128)(2,1)S(1)} reduce(bf16[128,1,1440]{2,1,0:T(2,128)(2,1)S(1)} %reshape_transpose_reshape_reshape.4, bf16[]{:T(256)} %broadcast.64), dimensions={1}, to_apply=%reshape_transpose_reshape_reshape.4.reduce_sub_computation | reduce | bytes 737282 | tf_op jit(solution)/shard_map/reshape;transpose;reshape;reshape | solution.py:39
  7.7 0.4 reshape.104
  8.2 44.1 %all_to_all.10 = bf16[128,2,720]{2,1,0:T(2,128)(2,1)S(1)} all-to-all(bf16[128,2,720]{2,1,0:T(2,128)(2,1)S(1)} %reshape.104), channel_id=1, replica_groups=mesh['groups'=2,'ep'=128] {'ep'}, dimensions={0} | all-to-all | bytes 737280 | tf_op jit(solution)/shard_map/all_to_all | solution.py:40
  52.3 0.7 reshape.105
  52.9 1.0 copy.29
  53.9 0.5 collective-permute-start
  54.4 1.5 %collective-permute-done = bf16[128,1,1440]{0,2,1:T(8,128)(2,1)S(1)} collective-permute-done((bf16[128,1,1440]{0,2,1:T(8,128)(2,1)S(1)}, bf16[128,1,1440]{0,2,1:T(8,128)(2,1)S(1)}, u32[]{:S(2)}, u32[]{:S(2)}) %collective-permute-start) | collective-permute-done | bytes 368672 | tf_op jit(solution)/shard_map/ppermute | solution.py:10
  55.9 0.1 broadcast_select_fusion.1
  56.0 3.5 %fusion.4 = f32[128,720]{0,1:T(8,128)S(1)} fusion(bf16[1,2880,720]{1,2,0:T(8,128)(2,1)} %param.11, bf16[128,1,1440]{0,2,1:T(8,128)(2,1)S(1)} %get-tuple-element.6, bf16[128,1,1440]{0,2,1:T(8,128)(2,1)S(1)} %get-tuple-element.5), kind=kOutput, calls=%fused_computation.4 | convolution fusion | flops 532316160 | bytes 5253120 | tf_op jit(solution)/shard_map/dot_general | solution.py:48
  59.5 8.2 %fusion.6 = bf16[128,2880]{0,1:T(8,128)(2,1)S(1)} fusion(bf16[1,720,2880]{2,1,0:T(8,128)(2,1)} %param.13, bf16[1,2880,720]{1,2,0:T(8,128)(2,1)} %param.12, bf16[128,1,1440]{0,2,1:T(8,128)(2,1)S(1)} %get-tuple-element.6, bf16[128,1,1440]{0,2,1:T(8,128)(2,1)S(1)} %get-tuple-element.5, f32[128,720]{0,1:T(8,128)S(1)} %fusion.4), kind=kOutput, calls=%fused_computation.6 | convolution fusion | flops 1064079360 | bytes 10137600 | tf_op jit(solution)/shard_map/dot_general | solution.py:51
  67.7 0.0 copy-start.1
  67.8 0.0 copy-start
  67.8 0.3 collective-permute-start.1
  68.1 1.5 %collective-permute-done.1 = bf16[128,1,1440]{0,2,1:T(8,128)(2,1)S(1)} collective-permute-done((bf16[128,1,1440]{0,2,1:T(8,128)(2,1)S(1)}, bf16[128,1,1440]{0,2,1:T(8,128)(2,1)S(1)}, u32[]{:S(2)}, u32[]{:S(2)}) %collective-permute-start.1) | collective-permute-done | bytes 368672 | tf_op jit(solution)/shard_map/ppermute | solution.py:10
  69.6 0.1 fusion.18
  69.7 0.9 reduce.2
  70.6 0.2 copy.32
  70.8 1.2 %reshape.106 = bf16[128,2,720]{2,1,0:T(2,128)(2,1)} reshape(bf16[128,1440]{1,0:T(8,128)(2,1)S(1)} %copy.32) | data formatting | bytes 737280
  72.0 7.7 %all-to-all-start.1 = ((bf16[128,2,720]{2,1,0:T(2,128)(2,1)}), bf16[128,2,720]{2,1,0:T(2,128)(2,1)S(1)}, u32[]{:S(2)}, u32[]{:S(2)}) async-start(bf16[128,2,720]{2,1,0:T(2,128)(2,1)} %reshape.106), calls=%async_computation.1 | async-start | bytes 786432 | tf_op jit(solution)/shard_map/all_to_all | solution.py:60
  79.7 0.1 reduce_sum.39
  79.8 0.1 copy.26
  79.8 0.0 copy-done.1
  79.9 16.6 %all-to-all-done.1 = bf16[128,2,720]{2,1,0:T(2,128)(2,1)S(1)} async-done(((bf16[128,2,720]{2,1,0:T(2,128)(2,1)}), bf16[128,2,720]{2,1,0:T(2,128)(2,1)S(1)}, u32[]{:S(2)}, u32[]{:S(2)}) %all-to-all-start.1) | async-done | bytes 368672 | tf_op jit(solution)/shard_map/all_to_all | solution.py:60
  96.5 0.7 reshape.107
  97.2 2.6 %reduce = bf16[128,1440]{1,0:T(8,128)(2,1)S(1)} reduce(bf16[128,1,1440]{2,1,0:T(2,128)(2,1)S(1)} %reshape.107, bf16[]{:T(256)} %constant.38), dimensions={1}, to_apply=%all_to_all.7.reduce_sub_computation | reduce | bytes 737282 | tf_op jit(solution)/shard_map/all_to_all | solution.py:60
  99.8 0.3 reshape.101
  100.1 0.3 fusion.15
  100.3 0.0 copy-done
  100.3 0.6 fusion.28
  (6 shorter events, 0.1 us)
Async XLA Ops:
  53.9 2.0 %collective-permute-start = (bf16[128,1,1440]{0,2,1:T(8,128)(2,1)S(1)}, bf16[128,1,1440]{0,2,1:T(8,128)(2,1)S(1)}, u32[]{:S(2)}, u32[]{:S(2)}) collective-permute-start(bf16[128,1,1440]{0,2,1:T(8,128)(2,1)S(1)} %copy.29), channel_id=1, source_target_pairs={{0,1},{1,0},{2,3},{3,2},{4,5},{5,4},{6,7},{7,6},{8,9},{9,8},{10,11... | collective-permute-start | bytes 1105928 | tf_op jit(solution)/shard_map/ppermute | solution.py:10
  67.7 12.1 %copy-start.1 = (s32[8,4]{0,1:T(4,128)S(1)}, s32[8,4]{0,1:T(4,128)}, u32[]{:S(2)}) copy-start(s32[8,4]{0,1:T(4,128)} %param.10) | copy-start | bytes 388
  67.8 32.6 %copy-start = (bf16[8,2880]{1,0:T(8,128)(2,1)S(1)}, bf16[8,2880]{1,0:T(8,128)(2,1)}, u32[]{:S(2)}) copy-start(bf16[8,2880]{1,0:T(8,128)(2,1)} %param.7) | copy-start | bytes 138244
  67.8 1.8 %collective-permute-start.1 = (bf16[128,1,1440]{0,2,1:T(8,128)(2,1)S(1)}, bf16[128,1,1440]{0,2,1:T(8,128)(2,1)S(1)}, u32[]{:S(2)}, u32[]{:S(2)}) collective-permute-start(bf16[128,1,1440]{0,2,1:T(8,128)(2,1)S(1)} %select_bitcast_fusion), channel_id=1, source_target_pairs={{0,1},{1,0},{2,3},{3,2},{4,5},{5,4},{6,7},{7,6},{8,9},{9,8},{10,11... | collective-permute-start | bytes 1105928 | tf_op jit(solution)/shard_map/ppermute | solution.py:10
  72.0 24.5 %all-to-all-start.1 = ((bf16[128,2,720]{2,1,0:T(2,128)(2,1)}), bf16[128,2,720]{2,1,0:T(2,128)(2,1)S(1)}, u32[]{:S(2)}, u32[]{:S(2)}) async-start(bf16[128,2,720]{2,1,0:T(2,128)(2,1)} %reshape.106), calls=%async_computation.1 | async-start | bytes 786432 | tf_op jit(solution)/shard_map/all_to_all | solution.py:60
where the time goes:
time: 101 us
  blocking collectives  44.1 us (44%)
  waiting for transfers between devices  19.7 us (20%)
  matrix products  12.2 us (12%)
  other arithmetic  9.73 us (10%)
  starting transfers between devices  8.45 us (8%)
  local copies, waits for them, and re-layouts  6.66 us (7%)
    all_to_all x1, blocking collectives, shards(): lax.all_to_all(outgoing, 'ep', split_axis=0, concat_axis=0, tiled=True)  44.1 us
    all_to_all x1, waiting for transfers between devices, shards(): lax.all_to_all(summed, 'ep', split_axis=0, concat_axis=0, tiled=True)  16.6 us
    dot_general x1, matrix products, shards(): jnp.dot(hidden, w_down[0], preferred_element_type=jnp.float32)  8.21 us
    all_to_all x1, starting transfers between devices, shards(): lax.all_to_all(summed, 'ep', split_axis=0, concat_axis=0, tiled=True)  7.67 us
    unnamed x10, local copies, waits for them, and re-layouts  3.91 us
    dot_general x1, matrix products, shards(): jnp.dot(token_rows, w_gate[0], preferred_element_type=jnp.float32)  3.52 us
    another operation x1, other arithmetic, shards(): jnp.transpose(outgoing, (0, 2, 1, 3)).reshape(devices, capacity, half_width)  3.22 us
    ppermute x2, waiting for transfers between devices, from_partner(): lax.ppermute(array, axis, [(i, i ^ 1 << bit) for i in range(lax.axis_size...  3.03 us
  transfers between devices with their start and end apart: 3, of which 3 were waited for; matrix products, arithmetic and copies ran while one was open for 0% of the time, Pallas kernels for 0%

commit v1 on v0

v1 whole, which is shorter than its diff:
```python
import functools
import math

import jax
import jax.numpy as jnp
from jax import lax
from jax.experimental import pallas as pl
from jax.experimental.pallas import tpu as pltpu
from jax.sharding import PartitionSpec as P

epsilon = 1e-05
MESH = pl.DeviceIdType.MESH
F32 = jnp.float32
BF16 = jnp.bfloat16


def order_of(side):
    return sorted(range(1, side), key=lambda d: -min(d, side - d))


def kernel(
    side,
    tokens_hbm, gain_hbm, ids_hbm, codes_hbm, gate_hbm, up_hbm, down_hbm,
    out_ref,
    tokens_v, gain_v, ids_v, codes_v, gate_v, up_v, down_v,
    picked, relayed, turned, mine, other, given, taken, summed, back, unturned, results,
    load_sem, weight_sem,
    send1, recv1, send2, recv2, send_x, recv_x, send_y, recv_y, send3, recv3, send4, recv4,
):
    me = lax.axis_index("ep")
    core = lax.rem(me, 2)
    chip = me // 2
    row, column = chip // side, lax.rem(chip, side)
    p = jnp.where(core == 0, column, row)
    q = jnp.where(core == 0, row, column)
    slots = side * side

    def device(p_of, q_of):
        y = jnp.where(core == 0, q_of, p_of)
        x = jnp.where(core == 0, p_of, q_of)
        return {"ep": (y * side + x) * 2 + core}

    partner = {"ep": me + 1 - 2 * core}
    far_first = order_of(side)

    small = [
        pltpu.make_async_copy(src, dst, load_sem.at[i])
        for i, (src, dst) in enumerate(
            [(tokens_hbm, tokens_v), (gain_hbm, gain_v), (ids_hbm, ids_v), (codes_hbm, codes_v)]
        )
    ]
    for copy in small:
        copy.start()
    weights = [
        pltpu.make_async_copy(src.at[0], dst, weight_sem.at[i])
        for i, (src, dst) in enumerate([(gate_hbm, gate_v), (up_hbm, up_v), (down_hbm, down_v)])
    ]

    barrier = pltpu.get_barrier_semaphore()
    for d in far_first:
        pl.semaphore_signal(barrier, inc=1, device_id=device(lax.rem(p + d, side), q), device_id_type=MESH)
        pl.semaphore_signal(barrier, inc=1, device_id=device(p, lax.rem(q + d, side)), device_id_type=MESH)
    pl.semaphore_signal(barrier, inc=1, device_id=partner, device_id_type=MESH)
    for copy in small:
        copy.wait()
    for copy in weights:
        copy.start()

    values = tokens_v[...].astype(F32)
    normed = values * lax.rsqrt(jnp.mean(values * values, axis=1, keepdims=True) + epsilon) * gain_v[...]
    normed = normed.astype(BF16)
    lane = lax.broadcasted_iota(jnp.int32, (tokens_v.shape[0], slots), 1)
    minor, major = lax.rem(lane, side), lane // side
    expert = jnp.where(core == 0, minor * side + major, lane)
    codes = codes_v[...].astype(F32)
    share = codes / jnp.sum(codes, axis=1, keepdims=True)
    chosen = jnp.zeros(lane.shape, F32)
    mix = jnp.zeros(lane.shape, F32)
    for k in range(ids_v.shape[1]):
        hit = ids_v[:, k : k + 1] == expert
        chosen = jnp.where(hit, 1.0, chosen)
        mix = jnp.where(hit, share[:, k : k + 1], mix)
    rows = lax.dot_general(
        chosen.astype(BF16), normed, (((0,), (0,)), ((), ())), preferred_element_type=F32
    )
    picked[...] = rows.astype(BF16).reshape(picked.shape)

    a = lax.broadcasted_iota(jnp.int32, (slots, slots), 0)
    b = lax.broadcasted_iota(jnp.int32, (slots, slots), 1)
    turn = jnp.where((a // side == lax.rem(b, side)) & (lax.rem(a, side) == b // side), 1.0, 0.0).astype(BF16)

    def turned_rows(ref):
        block = ref[...].reshape(slots, ref.shape[2])
        return jnp.dot(turn, block, preferred_element_type=F32).astype(BF16).reshape(ref.shape)

    pl.semaphore_wait(barrier, 2 * (side - 1) + 1)

    def scatter(src, dst, send, recv, place, device_of, own):
        copies = []
        for d in far_first:
            j = lax.rem(place + d, side)
            copy = pltpu.make_async_remote_copy(
                src_ref=src.at[j], dst_ref=dst.at[own], send_sem=send.at[j], recv_sem=recv.at[own],
                device_id=device_of(j), device_id_type=MESH,
            )
            copy.start()
            copies.append(copy)
        dst[own] = src[own]
        return copies

    def arrival(dst, send, recv, j):
        return pltpu.make_async_remote_copy(
            src_ref=dst.at[j], dst_ref=dst.at[j], send_sem=send.at[j], recv_sem=recv.at[j],
            device_id=partner, device_id_type=MESH,
        )

    near_first = far_first[::-1]
    along_p = lambda j: device(j, q)
    along_q = lambda j: device(p, j)
    sent = []
    sent += scatter(picked, relayed, send1, recv1, p, along_p, p)
    for d in near_first:
        arrival(relayed, send1, recv1, lax.rem(p + d, side)).wait_recv()
    turned[...] = turned_rows(relayed)
    sent += scatter(turned, mine, send2, recv2, q, along_q, q)

    for d in [0] + near_first:
        j = lax.rem(q + d, side)
        if d:
            arrival(mine, send2, recv2, j).wait_recv()
        copy = pltpu.make_async_remote_copy(
            src_ref=mine.at[j], dst_ref=other.at[j], send_sem=send_x.at[j], recv_sem=recv_x.at[j],
            device_id=partner, device_id_type=MESH,
        )
        copy.start()
        sent.append(copy)
    for copy in weights[:2]:
        copy.wait()
    for d in [0] + near_first:
        arrival(other, send_x, recv_x, lax.rem(q + d, side)).wait_recv()

    width = tokens_v.shape[1]
    arrived = jnp.concatenate([mine[...].reshape(slots, width), other[...].reshape(slots, width)], axis=0)
    gate_out = jnp.dot(arrived, gate_v[...], preferred_element_type=F32)
    upward = jnp.dot(arrived, up_v[...], preferred_element_type=F32)
    hidden = (gate_out / (1.0 + jnp.exp(-gate_out)) * upward).astype(BF16)
    weights[2].wait()
    partial = jnp.dot(hidden, down_v[...], preferred_element_type=F32).astype(BF16)
    given[...] = partial[slots:].reshape(given.shape)
    copy = pltpu.make_async_remote_copy(
        src_ref=given, dst_ref=taken, send_sem=send_y, recv_sem=recv_y, device_id=partner, device_id_type=MESH,
    )
    copy.start()
    copy.wait_recv()
    sent.append(copy)
    total = partial[:slots].astype(F32) + taken[...].reshape(slots, width).astype(F32)
    summed[...] = total.astype(BF16).reshape(summed.shape)

    sent += scatter(summed, back, send3, recv3, q, along_q, q)
    for d in near_first:
        arrival(back, send3, recv3, lax.rem(q + d, side)).wait_recv()
    unturned[...] = turned_rows(back)
    sent += scatter(unturned, results, send4, recv4, p, along_p, p)
    for d in near_first:
        arrival(results, send4, recv4, lax.rem(p + d, side)).wait_recv()
    block = results[...].reshape(slots, width)
    high = mix.astype(BF16)
    rest = mix - high.astype(F32)
    middle = rest.astype(BF16)
    low = (rest - middle.astype(F32)).astype(BF16)
    mixture = sum(jnp.dot(part, block, preferred_element_type=F32) for part in (low, middle, high))
    out_ref[...] = (tokens_v[...].astype(F32) + mixture).astype(BF16)
    for copy in sent:
        copy.wait_send()


def shards(tokens, norm_gain, expert_ids, gate_codes, w_gate, w_up, w_down):
    side = math.isqrt(lax.axis_size("ep") // 2)
    count, width = tokens.shape
    shard_ff = w_gate.shape[2]
    blocks = pltpu.VMEM((side, side, width), BF16)
    DMA = pltpu.SemaphoreType.DMA
    return pl.pallas_call(
        functools.partial(kernel, side),
        out_shape=jax.ShapeDtypeStruct((count, width), BF16),
        in_specs=[pl.BlockSpec(memory_space=pl.ANY)] * 7,
        out_specs=pl.BlockSpec(memory_space=pltpu.VMEM),
        scratch_shapes=[
            pltpu.VMEM((count, width), BF16),
            pltpu.VMEM((1, width), F32),
            pltpu.VMEM(expert_ids.shape, jnp.int32),
            pltpu.VMEM(gate_codes.shape, jnp.int32),
            pltpu.VMEM((width, shard_ff), BF16),
            pltpu.VMEM((width, shard_ff), BF16),
            pltpu.VMEM((shard_ff, width), BF16),
        ]
        + [blocks] * 11
        + [DMA((4,)), DMA((3,))]
        + [DMA((side,))] * 6
        + [DMA, DMA]
        + [DMA((side,))] * 4,
        compiler_params=pltpu.CompilerParams(
            collective_id=0, has_side_effects=True, vmem_limit_bytes=60 * 2**20
        ),
    )(tokens, norm_gain.reshape(1, width), expert_ids, gate_codes, w_gate, w_up, w_down)


def solution(mesh):
    return jax.shard_map(
        shards,
        mesh=mesh,
        in_specs=(
            P(("groups", "ep"), None),
            P(),
            P(("groups", "ep"), None),
            P(("groups", "ep"), None),
            P("ep", None, None),
            P("ep", None, None),
            P("ep", None, None),
        ),
        out_specs=P(("groups", "ep"), None),
        check_vma=False,
    )
```

time: 101 us -> 76.3 us (0.76); the launches traced: 101 us -> 75.1 us
  Pallas kernels: 0 us -> 56.6 us
  blocking collectives: 44.1 us -> 0 us
  waiting for transfers between devices: 19.7 us -> 0 us
  matrix products: 12.2 us -> 0 us
  local copies, waits for them, and re-layouts: 6.66 us -> 18.4 us
  other arithmetic: 9.73 us -> 0 us
  starting transfers between devices: 8.45 us -> 0 us
    pallas_call x0 -> x1, Pallas kernels: none -> 56.6 us  [shards(): pl.pallas_call(functools.partial(kernel, side), out_shape=jax.ShapeDtypeS...]
    all_to_all x1 -> x0, blocking collectives: 44.1 us -> none  [shards(): lax.all_to_all(outgoing, 'ep', split_axis=0, concat_axis=0, tiled=True)]
    all_to_all x1 -> x0, waiting for transfers between devices: 16.6 us -> none  [shards(): lax.all_to_all(summed, 'ep', split_axis=0, concat_axis=0, tiled=True)]
    unnamed x10 -> x5, local copies, waits for them, and re-layouts: 3.91 us -> 17.1 us
    dot_general x4 -> x0, matrix products: 12.2 us -> none  [the longest x1 8.21 us: shards(): jnp.dot(hidden, w_down[0], preferred_element_type=jnp.float32)]
    all_to_all x1 -> x0, starting transfers between devices: 7.67 us -> none  [shards(): lax.all_to_all(summed, 'ep', split_axis=0, concat_axis=0, tiled=True)]
    another operation x2 -> x0, other arithmetic: 3.28 us -> none  [the longest x1 3.22 us: shards(): jnp.transpose(outgoing, (0, 2, 1, 3)).reshape(devices, capacity, half_width)]
    ppermute x2 -> x0, waiting for transfers between devices: 3.03 us -> none  [from_partner(): lax.ppermute(array, axis, [(i, i ^ 1 << bit) for i in range(lax.axis_size...]
  transfers between devices with their start and end apart: 3 -> 0, of which waited for: 3 -> 0; matrix products, arithmetic and copies ran while one was open for 0% -> 0% of each run, Pallas kernels for 0% -> 0%
where the time goes in v1:
time: 76.3 us; the launch traced here: 75.1 us
  Pallas kernels  56.6 us (74%)
  local copies, waits for them, and re-layouts  18.4 us (24%)
    pallas_call x1, Pallas kernels, shards(): pl.pallas_call(functools.partial(kernel, side), out_shape=jax.ShapeDtypeS...  56.6 us
    unnamed x5, local copies, waits for them, and re-layouts  17.1 us

profile of v1, /device:TPU:513, one launch (start us, length us, event | category | flops | bytes accessed | tf_op | source)
XLA Modules:
  0.0 75.1 jit_solution(7161553769028305625)
XLA Ops:
  0.0 1.3 %copy.8.ids_hbm = s32[8,4]{1,0:T(8,128)} copy(s32[8,4]{0,1:T(4,128)} %param.9) | data formatting | bytes 256 | tf_op args[2]
  1.3 1.3 %copy.9.codes_hbm = s32[8,4]{1,0:T(8,128)} copy(s32[8,4]{0,1:T(4,128)} %param.10) | data formatting | bytes 256 | tf_op args[3]
  2.7 1.3 %reshape.3.gain_hbm = f32[1,2880]{1,0:T(1,128)} reshape(f32[2880]{0:T(1024)} %param.8) | data formatting | bytes 23040 | tf_op jit(solution)/shard_map/reshape | solution.py:205
  4.0 6.5 %copy.10.gate_hbm = bf16[1,2880,720]{2,1,0:T(8,128)(2,1)} copy(bf16[1,2880,720]{1,2,0:T(8,128)(2,1)} %param.11) | data formatting | bytes 8294400 | tf_op args[4]
  10.5 6.5 %copy.11.up_hbm = bf16[1,2880,720]{2,1,0:T(8,128)(2,1)} copy(bf16[1,2880,720]{1,2,0:T(8,128)(2,1)} %param.12) | data formatting | bytes 8294400 | tf_op args[5]
  17.0 56.6 %shard_map.73 = bf16[8,2880]{1,0:T(8,128)(2,1)} custom-call(bf16[8,2880]{1,0:T(8,128)(2,1)} %tokens_hbm.1, f32[1,2880]{1,0:T(1,128)} %reshape.3.gain_hbm, s32[8,4]{1,0:T(8,128)} %copy.8.ids_hbm, s32[8,4]{1,0:T(8,128)} %copy.9.codes_hbm, bf16[1,2880,720]{2,1,0:T(8,128)(2,1)} %copy.10.gate_hbm, bf16[1,2880,720]{2,1,0:T(8,128)(2,1)} %copy.11.up_hbm, ...), custom_call_target="tpu_custom_call" | custom-call | tf_op jit(solution)/shard_map/pallas_call | solution.py:183
  73.7 1.4 %copy.13 = bf16[8,2880]{1,0:T(8,128)(2,1)} copy(bf16[8,2880]{1,0:T(8,128)(2,1)} %shard_map.73) | data formatting | bytes 92160

commit v2 on v1

--- a/solution.py
+++ b/solution.py
@@ -12,6 +12,8 @@
 MESH = pl.DeviceIdType.MESH
 F32 = jnp.float32
 BF16 = jnp.bfloat16
+ROWS_BY_ROWS = (((1,), (1,)), ((), ()))
+COLUMNS_BY_ROWS = (((0,), (0,)), ((), ()))
 
 
 def order_of(side):
@@ -67,22 +69,20 @@
         copy.start()
 
     values = tokens_v[...].astype(F32)
-    normed = values * lax.rsqrt(jnp.mean(values * values, axis=1, keepdims=True) + epsilon) * gain_v[...]
+    normed = values * lax.rsqrt(jnp.mean(values * values, axis=1, keepdims=True) + epsilon) * gain_v[...].reshape(1, -1)
     normed = normed.astype(BF16)
-    lane = lax.broadcasted_iota(jnp.int32, (tokens_v.shape[0], slots), 1)
-    minor, major = lax.rem(lane, side), lane // side
-    expert = jnp.where(core == 0, minor * side + major, lane)
+    slot = lax.broadcasted_iota(jnp.int32, (slots, tokens_v.shape[0]), 0)
+    minor, major = lax.rem(slot, side), slot // side
+    expert = jnp.where(core == 0, minor * side + major, slot)
     codes = codes_v[...].astype(F32)
-    share = codes / jnp.sum(codes, axis=1, keepdims=True)
-    chosen = jnp.zeros(lane.shape, F32)
-    mix = jnp.zeros(lane.shape, F32)
-    for k in range(ids_v.shape[1]):
-        hit = ids_v[:, k : k + 1] == expert
+    share = codes / jnp.sum(codes, axis=0, keepdims=True)
+    chosen = jnp.zeros(slot.shape, F32)
+    mix = jnp.zeros(slot.shape, F32)
+    for k in range(ids_v.shape[0]):
+        hit = ids_v[k : k + 1, :] == expert
         chosen = jnp.where(hit, 1.0, chosen)
-        mix = jnp.where(hit, share[:, k : k + 1], mix)
-    rows = lax.dot_general(
-        chosen.astype(BF16), normed, (((0,), (0,)), ((), ())), preferred_element_type=F32
-    )
+        mix = jnp.where(hit, share[k : k + 1, :], mix)
+    rows = jnp.dot(chosen.astype(BF16), normed, preferred_element_type=F32)
     picked[...] = rows.astype(BF16).reshape(picked.shape)
 
     a = lax.broadcasted_iota(jnp.int32, (slots, slots), 0)
@@ -141,11 +141,11 @@
 
     width = tokens_v.shape[1]
     arrived = jnp.concatenate([mine[...].reshape(slots, width), other[...].reshape(slots, width)], axis=0)
-    gate_out = jnp.dot(arrived, gate_v[...], preferred_element_type=F32)
-    upward = jnp.dot(arrived, up_v[...], preferred_element_type=F32)
+    gate_out = lax.dot_general(gate_v[...], arrived, ROWS_BY_ROWS, preferred_element_type=F32)
+    upward = lax.dot_general(up_v[...], arrived, ROWS_BY_ROWS, preferred_element_type=F32)
     hidden = (gate_out / (1.0 + jnp.exp(-gate_out)) * upward).astype(BF16)
     weights[2].wait()
-    partial = jnp.dot(hidden, down_v[...], preferred_element_type=F32).astype(BF16)
+    partial = lax.dot_general(hidden, down_v[...], COLUMNS_BY_ROWS, preferred_element_type=F32).astype(BF16)
     given[...] = partial[slots:].reshape(given.shape)
     copy = pltpu.make_async_remote_copy(
         src_ref=given, dst_ref=taken, send_sem=send_y, recv_sem=recv_y, device_id=partner, device_id_type=MESH,
@@ -168,7 +168,9 @@
     rest = mix - high.astype(F32)
     middle = rest.astype(BF16)
     low = (rest - middle.astype(F32)).astype(BF16)
-    mixture = sum(jnp.dot(part, block, preferred_element_type=F32) for part in (low, middle, high))
+    mixture = sum(
+        lax.dot_general(part, block, COLUMNS_BY_ROWS, preferred_element_type=F32) for part in (low, middle, high)
+    )
     out_ref[...] = (tokens_v[...].astype(F32) + mixture).astype(BF16)
     for copy in sent:
         copy.wait_send()
@@ -187,11 +189,11 @@
         out_specs=pl.BlockSpec(memory_space=pltpu.VMEM),
         scratch_shapes=[
             pltpu.VMEM((count, width), BF16),
-            pltpu.VMEM((1, width), F32),
-            pltpu.VMEM(expert_ids.shape, jnp.int32),
-            pltpu.VMEM(gate_codes.shape, jnp.int32),
-            pltpu.VMEM((width, shard_ff), BF16),
-            pltpu.VMEM((width, shard_ff), BF16),
+            pltpu.VMEM((width,), F32),
+            pltpu.VMEM(expert_ids.shape[::-1], jnp.int32),
+            pltpu.VMEM(gate_codes.shape[::-1], jnp.int32),
+            pltpu.VMEM((shard_ff, width), BF16),
+            pltpu.VMEM((shard_ff, width), BF16),
             pltpu.VMEM((shard_ff, width), BF16),
         ]
         + [blocks] * 11
@@ -202,7 +204,10 @@
         compiler_params=pltpu.CompilerParams(
             collective_id=0, has_side_effects=True, vmem_limit_bytes=60 * 2**20
         ),
-    )(tokens, norm_gain.reshape(1, width), expert_ids, gate_codes, w_gate, w_up, w_down)
+    )(
+        tokens, norm_gain, expert_ids.T, gate_codes.T,
+        jnp.swapaxes(w_gate, 1, 2), jnp.swapaxes(w_up, 1, 2), w_down,
+    )
 
 
 def solution(mesh):

time: 76.3 us -> 60 us (0.79)
  local copies, waits for them, and re-layouts: 18.4 us -> 1.42 us
  Pallas kernels: 56.6 us -> 57.7 us
    unnamed x5 -> x1, local copies, waits for them, and re-layouts: 17.1 us -> 1.42 us
    reshape x1 -> x0, local copies, waits for them, and re-layouts: 1.31 us -> none  [shards(): norm_gain.reshape(1, width)]
    pallas_call x1, Pallas kernels: 56.6 us -> 57.7 us  [shards(): pl.pallas_call(functools.partial(kernel, side), out_shape=jax.ShapeDtypeS...]
where the time goes in v2:
time: 60 us; the launch traced here: 59.2 us
  Pallas kernels  57.7 us (96%)
  local copies, waits for them, and re-layouts  1.42 us (2%)
    pallas_call x1, Pallas kernels, shards(): pl.pallas_call(functools.partial(kernel, side), out_shape=jax.ShapeDtypeS...  57.7 us
    unnamed x1, local copies, waits for them, and re-layouts  1.42 us

profile of v2, /device:TPU:513, one launch (start us, length us, event | category | flops | bytes accessed | tf_op | source)
XLA Modules:
  0.0 59.2 jit_solution(12900602471759892027)
XLA Ops:
  0.0 57.7 %shard_map.73 = bf16[8,2880]{1,0:T(8,128)(2,1)} custom-call(bf16[8,2880]{1,0:T(8,128)(2,1)} %tokens_hbm.1, f32[2880]{0:T(1024)} %gain_hbm.1, s32[4,8]{1,0:T(4,128)} %bitcast.6, s32[4,8]{1,0:T(4,128)} %bitcast.7, bf16[1,720,2880]{2,1,0:T(8,128)(2,1)} %bitcast.4, bf16[1,720,2880]{2,1,0:T(8,128)(2,1)} %bitcast.5, bf16[1,720,2880]{2,1,0:T(8,128)(2,1)} %down_hbm.1), custom_call_target="tpu_custom_call" | custom-call | tf_op jit(solution)/shard_map/pallas_call | solution.py:185
  57.8 1.4 %copy.9 = bf16[8,2880]{1,0:T(8,128)(2,1)} copy(bf16[8,2880]{1,0:T(8,128)(2,1)} %shard_map.73) | data formatting | bytes 92160

commit v3 on v2

v3 whole, which is shorter than its diff:
```python
import functools
import math

import jax
import jax.numpy as jnp
from jax import lax
from jax.experimental import pallas as pl
from jax.experimental.pallas import tpu as pltpu
from jax.sharding import PartitionSpec as P

epsilon = 1e-05
MESH = pl.DeviceIdType.MESH
F32 = jnp.float32
BF16 = jnp.bfloat16
LANES = 128
ROWS_BY_ROWS = (((1,), (1,)), ((), ()))
COLUMNS_BY_ROWS = (((0,), (0,)), ((), ()))


def kernel(
    side, tiles,
    tokens_hbm, gain_hbm, ids_hbm, codes_hbm, gate_hbm, up_hbm, down_hbm,
    out_ref,
    tokens_v, gain_v, ids_v, ids_s, codes_s, gate_v, up_v, down_v,
    wide, picked, mine, other, arrived, given, taken, own_share, summed, results,
    load_sem, weight_sem,
    send1, recv1, send_x, recv_x, send_y, recv_y, send2, recv2,
):
    me = lax.axis_index("ep")
    core = lax.rem(me, 2)
    chip = me // 2
    row, column = chip // side, lax.rem(chip, side)
    chips = side * side
    count, width = tokens_v.shape
    top = ids_v.shape[0]
    padded = tiles * LANES
    used = pl.cdiv(width, LANES)
    partner = {"ep": me + 1 - 2 * core}

    near = lambda d: min(d, side - d)
    offsets = [(dy, dx) for dy in range(side) for dx in range(side) if dy or dx]
    offsets.sort(key=lambda o: -(near(o[0]) + near(o[1])))
    rows_at = [lax.rem(row + d, side) * side for d in range(side)]
    columns_at = [lax.rem(column + d, side) for d in range(side)]
    peers = [rows_at[dy] + columns_at[dx] for dy, dx in offsets]

    small = [
        pltpu.make_async_copy(src, dst, load_sem.at[i])
        for i, (src, dst) in enumerate(
            [(tokens_hbm, tokens_v), (gain_hbm, gain_v), (ids_hbm, ids_v), (ids_hbm, ids_s), (codes_hbm, codes_s)]
        )
    ]
    for copy in small:
        copy.start()
    weights = [
        pltpu.make_async_copy(src.at[0], dst, weight_sem.at[i])
        for i, (src, dst) in enumerate([(gate_hbm, gate_v), (up_hbm, up_v), (down_hbm, down_v)])
    ]

    barrier = pltpu.get_barrier_semaphore()
    for j in peers:
        pl.semaphore_signal(barrier, inc=1, device_id={"ep": 2 * j + core}, device_id_type=MESH)
    pl.semaphore_signal(barrier, inc=1, device_id=partner, device_id_type=MESH)
    for copy in small:
        copy.wait()
    for copy in weights:
        copy.start()

    values = tokens_v[...].astype(F32)
    normed = values * lax.rsqrt(jnp.mean(values * values, axis=1, keepdims=True) + epsilon) * gain_v[...].reshape(1, -1)
    normed = normed.astype(BF16)
    expert = lax.broadcasted_iota(jnp.int32, (chips, count), 0)
    chosen = jnp.zeros(expert.shape, F32)
    for k in range(top):
        chosen = jnp.where(ids_v[k : k + 1, :] == expert, 1.0, chosen)
    rows = jnp.dot(chosen.astype(BF16), normed, preferred_element_type=F32)

    def spread(value, base):
        n = value.shape[0]
        value = jnp.concatenate([value, jnp.zeros((n, padded - width), F32)], axis=1)
        for j in range(tiles):
            wide[pl.ds(base + j, n, stride=tiles), :] = value[:, j * LANES : (j + 1) * LANES]

    def spread_rows(base, n):
        return wide[pl.ds(base, n * tiles), :].reshape(n, tiles, LANES)

    spread(rows, 0)
    picked[...] = spread_rows(0, chips).astype(BF16)
    mine[chip] = picked[chip]

    pl.semaphore_wait(barrier, len(peers) + 1)

    def scatter(src, dst, send, recv):
        copies = []
        for j in peers:
            copy = pltpu.make_async_remote_copy(
                src_ref=src.at[j], dst_ref=dst.at[chip], send_sem=send.at[j], recv_sem=recv.at[chip],
                device_id={"ep": 2 * j + core}, device_id_type=MESH,
            )
            copy.start()
            copies.append(copy)
        return copies

    def arrival(dst, send, recv, j):
        return pltpu.make_async_remote_copy(
            src_ref=dst.at[j], dst_ref=dst.at[j], send_sem=send.at[j], recv_sem=recv.at[j],
            device_id=partner, device_id_type=MESH,
        )

    sent = scatter(picked, mine, send1, recv1)

    half = side // 2
    group = 2 * side
    order = sorted(range(half), key=lambda d: min(d, half - d))
    groups = [lax.rem(row // 2 + d, half) for d in order]

    def flatten(src, g, first):
        start = pl.multiple_of(g * group, group)
        place = pl.multiple_of(first + start, group)
        base = pl.multiple_of(place * tiles, group)
        wide[pl.ds(base, group * tiles), :] = src[pl.ds(start, group)].astype(F32).reshape(group * tiles, LANES)
        for j in range(used):
            lane_tile = wide[pl.ds(base + j, group, stride=tiles), :]
            arrived[pl.ds(place, group), j * LANES : (j + 1) * LANES] = lane_tile.astype(BF16)

    forwards = []
    for d, g in zip(order, groups):
        start = pl.multiple_of(g * group, group)
        for i in range(group):
            j = start + i

            if d == 0:
                @pl.when(j != chip)
                def _():
                    arrival(mine, send1, recv1, j).wait_recv()
            else:
                arrival(mine, send1, recv1, j).wait_recv()
        copy = pltpu.make_async_remote_copy(
            src_ref=mine.at[pl.ds(start, group)], dst_ref=other.at[pl.ds(start, group)],
            send_sem=send_x.at[g], recv_sem=recv_x.at[g], device_id=partner, device_id_type=MESH,
        )
        copy.start()
        forwards.append(copy)
        flatten(mine, g, 0)
    for copy, g in zip(forwards, groups):
        copy.wait_recv()
        flatten(other, g, chips)
    sent += forwards

    for copy in weights[:2]:
        copy.wait()
    rows_in = arrived[:, :width]
    gate_out = lax.dot_general(gate_v[...], rows_in, ROWS_BY_ROWS, preferred_element_type=F32)
    upward = lax.dot_general(up_v[...], rows_in, ROWS_BY_ROWS, preferred_element_type=F32)
    hidden = (gate_out / (1.0 + jnp.exp(-gate_out)) * upward).astype(BF16)
    weights[2].wait()
    pieces = given.shape[0]
    piece = given.shape[2]
    exchanges = []
    for i in range(pieces):
        low, size = i * piece, min(piece, width - i * piece)
        partial = lax.dot_general(
            hidden, down_v[:, low : low + size], COLUMNS_BY_ROWS, preferred_element_type=F32
        ).astype(BF16)
        given[i, :, :size] = partial[chips:]
        if size < piece:
            given[i, :, size:] = jnp.zeros((chips, piece - size), BF16)
        own_share[i, :, :size] = partial[:chips]
        copy = pltpu.make_async_remote_copy(
            src_ref=given.at[i], dst_ref=taken.at[i], send_sem=send_y.at[i], recv_sem=recv_y.at[i],
            device_id=partner, device_id_type=MESH,
        )
        copy.start()
        exchanges.append(copy)
    for i, copy in enumerate(exchanges):
        copy.wait_recv()
        size = min(piece, width - i * piece)
        total = own_share[i].astype(F32) + taken[i].astype(F32)
        for j in range(pl.cdiv(size, LANES)):
            wide[pl.ds(i * (piece // LANES) + j, chips, stride=tiles), :] = total[:, j * LANES : (j + 1) * LANES]
    sent += exchanges
    summed[...] = spread_rows(0, chips).astype(BF16)
    results[chip] = summed[chip]
    sent += scatter(summed, results, send2, recv2)
    for j in peers[::-1]:
        arrival(results, send2, recv2, j).wait_recv()

    for t in range(count):
        codes = [codes_s[k, t] for k in range(top)]
        mixture = sum(
            results[ids_s[k, t]].astype(F32) * codes[k].astype(F32) for k in range(top)
        )
        mixture = mixture / jnp.full(mixture.shape, sum(codes).astype(F32))
        wide[t * tiles : (t + 1) * tiles, :] = mixture
    for j in range(used):
        low, size = j * LANES, min(LANES, width - j * LANES)
        lane_tile = wide[pl.ds(j, count, stride=tiles), :]
        out_ref[:, low : low + size] = (
            tokens_v[:, low : low + size].astype(F32) + lane_tile[:, :size]
        ).astype(BF16)
    for copy in sent:
        copy.wait_send()


def shards(tokens, norm_gain, expert_ids, gate_codes, w_gate, w_up, w_down):
    side = math.isqrt(lax.axis_size("ep") // 2)
    chips = side * side
    count, width = tokens.shape
    shard_ff = w_gate.shape[2]
    tiles = 8 * pl.cdiv(width, 8 * LANES)
    pieces = 3
    piece = LANES * (tiles // pieces)
    blocks = pltpu.VMEM((chips, tiles, LANES), BF16)
    shares = pltpu.VMEM((pieces, chips, piece), BF16)
    DMA = pltpu.SemaphoreType.DMA
    return pl.pallas_call(
        functools.partial(kernel, side, tiles),
        out_shape=jax.ShapeDtypeStruct((count, width), BF16),
        in_specs=[pl.BlockSpec(memory_space=pl.ANY)] * 7,
        out_specs=pl.BlockSpec(memory_space=pltpu.VMEM),
        scratch_shapes=[
            pltpu.VMEM((count, width), BF16),
            pltpu.VMEM((width,), F32),
            pltpu.VMEM(expert_ids.shape[::-1], jnp.int32),
            pltpu.SMEM(expert_ids.shape[::-1], jnp.int32),
            pltpu.SMEM(gate_codes.shape[::-1], jnp.int32),
            pltpu.VMEM((shard_ff, width), BF16),
            pltpu.VMEM((shard_ff, width), BF16),
            pltpu.VMEM((shard_ff, width), BF16),
            pltpu.VMEM((2 * chips * tiles, LANES), F32),
            blocks,
            blocks,
            blocks,
            pltpu.VMEM((2 * chips, tiles * LANES), BF16),
            shares,
            shares,
            shares,
            blocks,
            blocks,
            DMA((5,)),
            DMA((3,)),
            DMA((chips,)),
            DMA((chips,)),
            DMA((side // 2,)),
            DMA((side // 2,)),
            DMA((pieces,)),
            DMA((pieces,)),
            DMA((chips,)),
            DMA((chips,)),
        ],
        compiler_params=pltpu.CompilerParams(
            collective_id=0, has_side_effects=True, vmem_limit_bytes=60 * 2**20
        ),
    )(
        tokens, norm_gain, expert_ids.T, gate_codes.T,
        jnp.swapaxes(w_gate, 1, 2), jnp.swapaxes(w_up, 1, 2), w_down,
    )


def solution(mesh):
    return jax.shard_map(
        shards,
        mesh=mesh,
        in_specs=(
            P(("groups", "ep"), None),
            P(),
            P(("groups", "ep"), None),
            P(("groups", "ep"), None),
            P("ep", None, None),
            P("ep", None, None),
            P("ep", None, None),
        ),
        out_specs=P(("groups", "ep"), None),
        check_vma=False,
    )
```

time: 60 us -> 54.6 us (0.910)
  Pallas kernels: 57.7 us -> 52.5 us
    pallas_call x1, Pallas kernels: 57.7 us -> 52.5 us  [shards(): pl.pallas_call(functools.partial(kernel, side, tiles), out_shape=jax.Shap...]
where the time goes in v3:
time: 54.6 us; the launch traced here: 54 us
  Pallas kernels  52.5 us (96%)
  local copies, waits for them, and re-layouts  1.42 us (3%)
    pallas_call x1, Pallas kernels, shards(): pl.pallas_call(functools.partial(kernel, side, tiles), out_shape=jax.Shap...  52.5 us
    unnamed x1, local copies, waits for them, and re-layouts  1.42 us

profile of v3, /device:TPU:513, one launch (start us, length us, event | category | flops | bytes accessed | tf_op | source)
XLA Modules:
  0.0 54.0 jit_solution(5993141183296940944)
XLA Ops:
  0.0 52.5 %shard_map.73 = bf16[8,2880]{1,0:T(8,128)(2,1)} custom-call(bf16[8,2880]{1,0:T(8,128)(2,1)} %tokens_hbm.1, f32[2880]{0:T(1024)} %gain_hbm.1, s32[4,8]{1,0:T(4,128)} %bitcast.6, s32[4,8]{1,0:T(4,128)} %bitcast.7, bf16[1,720,2880]{2,1,0:T(8,128)(2,1)} %bitcast.4, bf16[1,720,2880]{2,1,0:T(8,128)(2,1)} %bitcast.5, bf16[1,720,2880]{2,1,0:T(8,128)(2,1)} %down_hbm.1), custom_call_target="tpu_custom_call" | custom-call | tf_op jit(solution)/shard_map/pallas_call | solution.py:216
  52.5 1.4 %copy.9 = bf16[8,2880]{1,0:T(8,128)(2,1)} copy(bf16[8,2880]{1,0:T(8,128)(2,1)} %shard_map.73) | data formatting | bytes 92160

commit v4 on v3

--- a/solution.py
+++ b/solution.py
@@ -39,10 +39,13 @@
 
     near = lambda d: min(d, side - d)
     offsets = [(dy, dx) for dy in range(side) for dx in range(side) if dy or dx]
-    offsets.sort(key=lambda o: -(near(o[0]) + near(o[1])))
-    rows_at = [lax.rem(row + d, side) * side for d in range(side)]
+    offsets.sort(key=lambda o: (-near(o[0]), -near(o[1])))
+    rows_at = [lax.rem(row + d, side) for d in range(side)]
     columns_at = [lax.rem(column + d, side) for d in range(side)]
-    peers = [rows_at[dy] + columns_at[dx] for dy, dx in offsets]
+    first_at = [jnp.where(core == 0, r * side, c) for r, c in zip(rows_at, columns_at)]
+    turned_first = [jnp.where(core == 0, column + d, (row + d)) for d in range(side)]
+    second_at = [lax.rem(v, side) * jnp.where(core == 0, 1, side) for v in turned_first]
+    peers = [first_at[a] + second_at[b] for a, b in offsets]
 
     small = [
         pltpu.make_async_copy(src, dst, load_sem.at[i])
@@ -124,6 +127,12 @@
             arrived[pl.ds(place, group), j * LANES : (j + 1) * LANES] = lane_tile.astype(BF16)
 
     forwards = []
+
+    def flatten_other():
+        i = len(forwards) - 1
+        forwards[i].wait_recv()
+        flatten(other, groups[i], chips)
+
     for d, g in zip(order, groups):
         start = pl.multiple_of(g * group, group)
         for i in range(group):
@@ -140,11 +149,11 @@
             send_sem=send_x.at[g], recv_sem=recv_x.at[g], device_id=partner, device_id_type=MESH,
         )
         copy.start()
+        if forwards:
+            flatten_other()
         forwards.append(copy)
         flatten(mine, g, 0)
-    for copy, g in zip(forwards, groups):
-        copy.wait_recv()
-        flatten(other, g, chips)
+    flatten_other()
     sent += forwards
 
     for copy in weights[:2]:
@@ -216,7 +225,7 @@
     return pl.pallas_call(
         functools.partial(kernel, side, tiles),
         out_shape=jax.ShapeDtypeStruct((count, width), BF16),
-        in_specs=[pl.BlockSpec(memory_space=pl.ANY)] * 7,
+        in_specs=[pl.BlockSpec(memory_space=pltpu.HBM)] * 7,
         out_specs=pl.BlockSpec(memory_space=pltpu.VMEM),
         scratch_shapes=[
             pltpu.VMEM((count, width), BF16),
@@ -249,12 +258,15 @@
             DMA((chips,)),
         ],
         compiler_params=pltpu.CompilerParams(
-            collective_id=0, has_side_effects=True, vmem_limit_bytes=60 * 2**20
+            collective_id=0, has_side_effects=True, vmem_limit_bytes=28 * 2**20
         ),
-    )(
-        tokens, norm_gain, expert_ids.T, gate_codes.T,
-        jnp.swapaxes(w_gate, 1, 2), jnp.swapaxes(w_up, 1, 2), w_down,
-    )
+    )(*[
+        pltpu.with_memory_space_constraint(array, pltpu.HBM)
+        for array in (
+            tokens, norm_gain, expert_ids.T, gate_codes.T,
+            jnp.swapaxes(w_gate, 1, 2), jnp.swapaxes(w_up, 1, 2), w_down,
+        )
+    ])
 
 
 def solution(mesh):

time: 54.6 us -> 55.8 us (1.022)
  Pallas kernels: 52.5 us -> 55.1 us
  local copies, waits for them, and re-layouts: 1.42 us -> 0.62 us
    pallas_call x1, Pallas kernels: 52.5 us -> 55.1 us  [shards(): pl.pallas_call(functools.partial(kernel, side, tiles), out_shape=jax.Shap...]
    unnamed x1, local copies, waits for them, and re-layouts: 1.42 us -> 0.62 us
where the time goes in v4:
time: 55.8 us; the launch traced here: 55.7 us
  Pallas kernels  55.1 us (99%)
  local copies, waits for them, and re-layouts  0.62 us (1%)
    pallas_call x1, Pallas kernels, shards(): pl.pallas_call(functools.partial(kernel, side, tiles), out_shape=jax.Shap...  55.1 us

profile of v4, /device:TPU:513, one launch (start us, length us, event | category | flops | bytes accessed | tf_op | source)
XLA Modules:
  0.0 55.7 jit_solution(11949362481723906507)
XLA Ops:
  0.0 55.1 %shard_map.73 = bf16[8,2880]{1,0:T(8,128)(2,1)S(1)} custom-call(bf16[8,2880]{1,0:T(8,128)(2,1)} %tokens_hbm.1, f32[2880]{0:T(1024)} %gain_hbm.1, s32[4,8]{1,0:T(4,128)} %bitcast.6, s32[4,8]{1,0:T(4,128)} %bitcast.7, bf16[1,720,2880]{2,1,0:T(8,128)(2,1)} %bitcast.4, bf16[1,720,2880]{2,1,0:T(8,128)(2,1)} %bitcast.5, bf16[1,720,2880]{2,1,0:T(8,128)(2,1)} %down_hbm.1), custom_call_target="tpu_custom_call" | custom-call | tf_op jit(solution)/shard_map/pallas_call | solution.py:225
  55.1 0.6 %copy.9 = bf16[8,2880]{1,0:T(8,128)(2,1)} copy(bf16[8,2880]{1,0:T(8,128)(2,1)S(1)} %shard_map.73) | data formatting | bytes 92160

commit v5 on v4

--- a/solution.py
+++ b/solution.py
@@ -39,13 +39,14 @@
 
     near = lambda d: min(d, side - d)
     offsets = [(dy, dx) for dy in range(side) for dx in range(side) if dy or dx]
-    offsets.sort(key=lambda o: (-near(o[0]), -near(o[1])))
     rows_at = [lax.rem(row + d, side) for d in range(side)]
     columns_at = [lax.rem(column + d, side) for d in range(side)]
-    first_at = [jnp.where(core == 0, r * side, c) for r, c in zip(rows_at, columns_at)]
-    turned_first = [jnp.where(core == 0, column + d, (row + d)) for d in range(side)]
-    second_at = [lax.rem(v, side) * jnp.where(core == 0, 1, side) for v in turned_first]
-    peers = [first_at[a] + second_at[b] for a, b in offsets]
+    offsets.sort(key=lambda o: -(near(o[0]) + near(o[1])))
+    peers_out = [rows_at[dy] * side + columns_at[dx] for dy, dx in offsets]
+    offsets.sort(key=lambda o: (-near(o[0]), -near(o[1])))
+    major = [jnp.where(core == 0, r * side, c) for r, c in zip(rows_at, columns_at)]
+    minor = [jnp.where(core == 0, c, r * side) for r, c in zip(rows_at, columns_at)]
+    peers_back = [major[i] + minor[j] for i, j in offsets]
 
     small = [
         pltpu.make_async_copy(src, dst, load_sem.at[i])
@@ -61,7 +62,7 @@
     ]
 
     barrier = pltpu.get_barrier_semaphore()
-    for j in peers:
+    for j in peers_out:
         pl.semaphore_signal(barrier, inc=1, device_id={"ep": 2 * j + core}, device_id_type=MESH)
     pl.semaphore_signal(barrier, inc=1, device_id=partner, device_id_type=MESH)
     for copy in small:
@@ -91,9 +92,9 @@
     picked[...] = spread_rows(0, chips).astype(BF16)
     mine[chip] = picked[chip]
 
-    pl.semaphore_wait(barrier, len(peers) + 1)
-
-    def scatter(src, dst, send, recv):
+    pl.semaphore_wait(barrier, len(peers_out) + 1)
+
+    def scatter(peers, src, dst, send, recv):
         copies = []
         for j in peers:
             copy = pltpu.make_async_remote_copy(
@@ -110,7 +111,7 @@
             device_id=partner, device_id_type=MESH,
         )
 
-    sent = scatter(picked, mine, send1, recv1)
+    sent = scatter(peers_out, picked, mine, send1, recv1)
 
     half = side // 2
     group = 2 * side
@@ -190,8 +191,8 @@
     sent += exchanges
     summed[...] = spread_rows(0, chips).astype(BF16)
     results[chip] = summed[chip]
-    sent += scatter(summed, results, send2, recv2)
-    for j in peers[::-1]:
+    sent += scatter(peers_back, summed, results, send2, recv2)
+    for j in peers_back[::-1]:
         arrival(results, send2, recv2, j).wait_recv()
 
     for t in range(count):

time: 55.8 us -> 55.4 us (level)
  no operation moved by 1% of the time
where the time goes in v5:
time: 55.4 us; the launch traced here: 55.3 us
  Pallas kernels  54.7 us (99%)
  local copies, waits for them, and re-layouts  0.62 us (1%)
    pallas_call x1, Pallas kernels, shards(): pl.pallas_call(functools.partial(kernel, side, tiles), out_shape=jax.Shap...  54.7 us

profile of v5, /device:TPU:513, one launch (start us, length us, event | category | flops | bytes accessed | tf_op | source)
XLA Modules:
  0.0 55.3 jit_solution(549141351443190824)
XLA Ops:
  0.0 54.7 %shard_map.73 = bf16[8,2880]{1,0:T(8,128)(2,1)S(1)} custom-call(bf16[8,2880]{1,0:T(8,128)(2,1)} %tokens_hbm.1, f32[2880]{0:T(1024)} %gain_hbm.1, s32[4,8]{1,0:T(4,128)} %bitcast.6, s32[4,8]{1,0:T(4,128)} %bitcast.7, bf16[1,720,2880]{2,1,0:T(8,128)(2,1)} %bitcast.4, bf16[1,720,2880]{2,1,0:T(8,128)(2,1)} %bitcast.5, bf16[1,720,2880]{2,1,0:T(8,128)(2,1)} %down_hbm.1), custom_call_target="tpu_custom_call" | custom-call | tf_op jit(solution)/shard_map/pallas_call | solution.py:226
  54.7 0.6 %copy.9 = bf16[8,2880]{1,0:T(8,128)(2,1)} copy(bf16[8,2880]{1,0:T(8,128)(2,1)S(1)} %shard_map.73) | data formatting | bytes 92160

commit v6 on v4

v6 whole, which is shorter than its diff:
```python
import functools
import math

import jax
import jax.numpy as jnp
from jax import lax
from jax.experimental import pallas as pl
from jax.experimental.pallas import tpu as pltpu
from jax.sharding import PartitionSpec as P

epsilon = 1e-05
MESH = pl.DeviceIdType.MESH
F32 = jnp.float32
BF16 = jnp.bfloat16
LANES = 128


def kernel(
    side, tiles,
    tokens_hbm, gain_hbm, ids_hbm, codes_hbm, gate_hbm, up_hbm, down_hbm,
    out_ref,
    tokens_v, gain_v, ids_v, ids_s, codes_s, gate_v, up_v, down_v, gate_t, up_t,
    picked, slots, arrived, share, taken, summed, results,
    load_sem, weight_sem, ready,
    send1, recv1, send_x, recv_x, send_y, recv_y, send2, recv2,
):
    me = lax.axis_index("ep")
    core = lax.rem(me, 2)
    chip = me // 2
    row, column = chip // side, lax.rem(chip, side)
    chips = side * side
    count, width = tokens_v.shape
    top = ids_v.shape[0]
    padded = tiles * LANES
    partner = {"ep": me + 1 - 2 * core}

    near = lambda d: min(d, side - d)
    offsets = [(dy, dx) for dy in range(side) for dx in range(side) if dy or dx]
    rows_at = [lax.rem(row + d, side) * side for d in range(side)]
    columns_at = [lax.rem(column + d, side) for d in range(side)]
    offsets.sort(key=lambda o: -(near(o[0]) + near(o[1])))
    peers = [rows_at[dy] + columns_at[dx] for dy, dx in offsets]

    small = [
        pltpu.make_async_copy(src, dst, load_sem.at[i])
        for i, (src, dst) in enumerate(
            [(tokens_hbm, tokens_v), (gain_hbm, gain_v), (ids_hbm, ids_v), (ids_hbm, ids_s), (codes_hbm, codes_s)]
        )
    ]
    for copy in small:
        copy.start()
    weights = [
        pltpu.make_async_copy(src.at[0], dst, weight_sem.at[i])
        for i, (src, dst) in enumerate([(gate_hbm, gate_v), (up_hbm, up_v), (down_hbm, down_v)])
    ]

    barrier = pltpu.get_barrier_semaphore()
    for j in peers:
        pl.semaphore_signal(barrier, inc=1, device_id={"ep": 2 * j + core}, device_id_type=MESH)

    @pl.when(core == 1)
    def _():
        pl.semaphore_signal(barrier, inc=1, device_id=partner, device_id_type=MESH)

    for copy in small:
        copy.wait()
    for copy in weights:
        copy.start()

    values = tokens_v[...].astype(F32)
    normed = values * lax.rsqrt(jnp.mean(values * values, axis=1, keepdims=True) + epsilon) * gain_v[...].reshape(1, -1)
    normed = normed.astype(BF16)
    expert = lax.broadcasted_iota(jnp.int32, (chips, count), 0)
    chosen = jnp.zeros(expert.shape, F32)
    for k in range(top):
        chosen = jnp.where(ids_v[k : k + 1, :] == expert, 1.0, chosen)
    rows = jnp.dot(chosen.astype(BF16), normed, preferred_element_type=F32)
    rows = jnp.concatenate([rows, jnp.zeros((chips, padded - width), F32)], axis=1)
    picked[...] = rows.reshape(picked.shape).astype(BF16)
    slots[core, chip] = picked[chip]

    pl.semaphore_wait(barrier, len(peers) + 1 - core)

    @pl.when(core == 0)
    def _():
        pl.semaphore_signal(ready, inc=1, device_id=partner, device_id_type=MESH)

    def scatter(src, dst, send, recv):
        for j in peers:
            pltpu.make_async_remote_copy(
                src_ref=src.at[j], dst_ref=dst.at[chip], send_sem=send.at[j], recv_sem=recv.at[chip],
                device_id={"ep": 2 * j + core}, device_id_type=MESH,
            ).start()

    def transfer(src, dst, send, recv):
        return pltpu.make_async_remote_copy(
            src_ref=src, dst_ref=dst, send_sem=send, recv_sem=recv, device_id=partner, device_id_type=MESH,
        )

    scatter(picked, slots.at[core], send1, recv1)

    depth = gate_t.shape[1]
    hidden_size = gate_v.shape[0]
    for i, (src, dst) in enumerate([(gate_v, gate_t), (up_v, up_t)]):
        weights[i].wait()
        dst[:, hidden_size:] = jnp.zeros((dst.shape[0], depth - hidden_size), BF16)
        for low in range(0, width, LANES):
            size = min(LANES, width - low)
            dst[low : low + size, :hidden_size] = src[:, low : low + size].T
        dst[width:, :] = jnp.zeros((dst.shape[0] - width, depth), BF16)

    half = side // 2
    group = 2 * side
    pieces, _, piece = share.shape[1:]
    sizes = [min(piece, width - i * piece) for i in range(pieces)]
    groups = [lax.rem(row // 2 + d, half) for d in sorted(range(half), key=lambda d: min(d, half - d))]

    def forward(plane, g):
        block = slots.at[plane, pl.ds(g * group, group)]
        return transfer(block, block, send_x.at[g], recv_x.at[g])

    def exchange(plane, i):
        return transfer(share.at[plane, i], taken.at[i], send_y.at[i], recv_y.at[i])

    def receive(plane):
        @pl.when(core == plane)
        def _():
            if plane == 1:
                pl.semaphore_wait(ready, 1)
            for n, g in enumerate(groups):
                for i in range(group):
                    j = g * group + i
                    block = slots.at[plane, j]

                    def arrive():
                        transfer(block, block, send1.at[j], recv1.at[j]).wait_recv()

                    if n == 0:
                        pl.when(j != chip)(arrive)
                    else:
                        arrive()
                forward(plane, g).start()

    for plane in (1, 0):
        receive(plane)

        @pl.when(core != plane)
        def _():
            for g in groups:
                forward(plane, g).wait_recv()

        arrived[...] = slots[plane].reshape(chips, padded)
        rows_in = arrived[:, : gate_t.shape[0]]
        gate_out = jnp.dot(rows_in, gate_t[...], preferred_element_type=F32)
        upward = jnp.dot(rows_in, up_t[...], preferred_element_type=F32)
        hidden = (gate_out / (1.0 + jnp.exp(-gate_out)) * upward).astype(BF16)[:, :hidden_size]
        if plane == 1:
            weights[2].wait()
        for i, size in enumerate(sizes):
            low = i * piece
            partial = jnp.dot(
                hidden, down_v[:, low : low + size], preferred_element_type=F32
            ).astype(BF16)
            if size < piece:
                partial = jnp.concatenate([partial, jnp.zeros((chips, piece - size), BF16)], axis=1)
            share[plane, i] = partial

            @pl.when(core != plane)
            def _():
                exchange(plane, i).start()

        @pl.when(core == plane)
        def _():
            for i in range(pieces):
                exchange(plane, i).wait_recv()
                total = share[plane, i].astype(F32) + taken[i].astype(F32)
                first = i * (piece // LANES)
                summed[:, first : first + piece // LANES, :] = total.reshape(
                    chips, piece // LANES, LANES
                ).astype(BF16)
            results[chip] = summed[chip]
            scatter(summed, results, send2, recv2)

    for j in peers[::-1]:
        transfer(results.at[j], results.at[j], send2.at[j], recv2.at[j]).wait_recv()

    mixtures = []
    for t in range(count):
        codes = [codes_s[k, t] for k in range(top)]
        mixture = sum(
            results[ids_s[k, t]].astype(F32) * codes[k].astype(F32) for k in range(top)
        )
        mixtures.append(mixture / jnp.full(mixture.shape, sum(codes).astype(F32)))
    mixture = jnp.stack(mixtures).reshape(count, padded)[:, :width]
    out_ref[...] = (tokens_v[...].astype(F32) + mixture).astype(BF16)

    for j in peers:
        transfer(picked.at[j], picked.at[j], send1.at[j], recv1.at[j]).wait_send()
        transfer(summed.at[j], summed.at[j], send2.at[j], recv2.at[j]).wait_send()
    for g in range(half):
        forward(core, g).wait_send()
    for i in range(pieces):
        exchange(1 - core, i).wait_send()


def shards(tokens, norm_gain, expert_ids, gate_codes, w_gate, w_up, w_down):
    side = math.isqrt(lax.axis_size("ep") // 2)
    chips = side * side
    count, width = tokens.shape
    shard_ff = w_gate.shape[2]
    tiles = 8 * pl.cdiv(width, 8 * LANES)
    pieces = 3
    piece = LANES * (tiles // pieces)
    blocks = pltpu.VMEM((chips, tiles, LANES), BF16)
    turned = pltpu.VMEM((LANES * pl.cdiv(width, LANES), 2 * LANES * pl.cdiv(shard_ff, 2 * LANES)), BF16)
    shares = (pieces, chips, piece)
    DMA = pltpu.SemaphoreType.DMA
    return pl.pallas_call(
        functools.partial(kernel, side, tiles),
        out_shape=jax.ShapeDtypeStruct((count, width), BF16),
        in_specs=[pl.BlockSpec(memory_space=pltpu.HBM)] * 7,
        out_specs=pl.BlockSpec(memory_space=pltpu.VMEM),
        scratch_shapes=[
            pltpu.VMEM((count, width), BF16),
            pltpu.VMEM((width,), F32),
            pltpu.VMEM(expert_ids.shape[::-1], jnp.int32),
            pltpu.SMEM(expert_ids.shape[::-1], jnp.int32),
            pltpu.SMEM(gate_codes.shape[::-1], jnp.int32),
            pltpu.VMEM((shard_ff, width), BF16),
            pltpu.VMEM((shard_ff, width), BF16),
            pltpu.VMEM((shard_ff, width), BF16),
            turned,
            turned,
            blocks,
            pltpu.VMEM((2, chips, tiles, LANES), BF16),
            pltpu.VMEM((chips, tiles * LANES), BF16),
            pltpu.VMEM((2,) + shares, BF16),
            pltpu.VMEM(shares, BF16),
            blocks,
            blocks,
            DMA((5,)),
            DMA((3,)),
            pltpu.SemaphoreType.REGULAR,
            DMA((chips,)),
            DMA((chips,)),
            DMA((side // 2,)),
            DMA((side // 2,)),
            DMA((pieces,)),
            DMA((pieces,)),
            DMA((chips,)),
            DMA((chips,)),
        ],
        compiler_params=pltpu.CompilerParams(
            collective_id=0, has_side_effects=True, vmem_limit_bytes=44 * 2**20
        ),
    )(*[
        pltpu.with_memory_space_constraint(array, pltpu.HBM)
        for array in (
            tokens, norm_gain, expert_ids.T, gate_codes.T,
            jnp.swapaxes(w_gate, 1, 2), jnp.swapaxes(w_up, 1, 2), w_down,
        )
    ])


def solution(mesh):
    return jax.shard_map(
        shards,
        mesh=mesh,
        in_specs=(
            P(("groups", "ep"), None),
            P(),
            P(("groups", "ep"), None),
            P(("groups", "ep"), None),
            P("ep", None, None),
            P("ep", None, None),
            P("ep", None, None),
        ),
        out_specs=P(("groups", "ep"), None),
        check_vma=False,
    )
```

time: 55.8 us -> 50.7 us (0.909)
  the two profiles are of different devices: /device:TPU:513 before, /device:TPU:640 now
where the time goes in v6:
time: 50.7 us; the launch traced here: 50.6 us
  Pallas kernels  50 us (99%)
  local copies, waits for them, and re-layouts  0.62 us (1%)
    pallas_call x1, Pallas kernels, shards(): pl.pallas_call(functools.partial(kernel, side, tiles), out_shape=jax.Shap...  50 us

profile of v6, /device:TPU:640, one launch (start us, length us, event | category | flops | bytes accessed | tf_op | source)
XLA Modules:
  0.0 50.6 jit_solution(18257907186730387544)
XLA Ops:
  0.0 50.0 %shard_map.73 = bf16[8,2880]{1,0:T(8,128)(2,1)S(1)} custom-call(bf16[8,2880]{1,0:T(8,128)(2,1)} %tokens_hbm.1, f32[2880]{0:T(1024)} %gain_hbm.1, s32[4,8]{1,0:T(4,128)} %bitcast.6, s32[4,8]{1,0:T(4,128)} %bitcast.7, bf16[1,720,2880]{2,1,0:T(8,128)(2,1)} %bitcast.4, bf16[1,720,2880]{2,1,0:T(8,128)(2,1)} %bitcast.5, bf16[1,720,2880]{2,1,0:T(8,128)(2,1)} %down_hbm.1), custom_call_target="tpu_custom_call" | custom-call | tf_op jit(solution)/shard_map/pallas_call | solution.py:218
  50.0 0.6 %copy.9 = bf16[8,2880]{1,0:T(8,128)(2,1)} copy(bf16[8,2880]{1,0:T(8,128)(2,1)S(1)} %shard_map.73) | data formatting | bytes 92160

commit v7 on v6

--- a/solution.py
+++ b/solution.py
@@ -41,6 +41,14 @@
     offsets.sort(key=lambda o: -(near(o[0]) + near(o[1])))
     peers = [rows_at[dy] + columns_at[dx] for dy, dx in offsets]
 
+    barrier = pltpu.get_barrier_semaphore()
+    for j in peers:
+        pl.semaphore_signal(barrier, inc=1, device_id={"ep": 2 * j + core}, device_id_type=MESH)
+
+    @pl.when(core == 1)
+    def _():
+        pl.semaphore_signal(barrier, inc=1, device_id=partner, device_id_type=MESH)
+
     small = [
         pltpu.make_async_copy(src, dst, load_sem.at[i])
         for i, (src, dst) in enumerate(
@@ -53,14 +61,6 @@
         pltpu.make_async_copy(src.at[0], dst, weight_sem.at[i])
         for i, (src, dst) in enumerate([(gate_hbm, gate_v), (up_hbm, up_v), (down_hbm, down_v)])
     ]
-
-    barrier = pltpu.get_barrier_semaphore()
-    for j in peers:
-        pl.semaphore_signal(barrier, inc=1, device_id={"ep": 2 * j + core}, device_id_type=MESH)
-
-    @pl.when(core == 1)
-    def _():
-        pl.semaphore_signal(barrier, inc=1, device_id=partner, device_id_type=MESH)
 
     for copy in small:
         copy.wait()
@@ -85,11 +85,11 @@
     def _():
         pl.semaphore_signal(ready, inc=1, device_id=partner, device_id_type=MESH)
 
-    def scatter(src, dst, send, recv):
-        for j in peers:
+    def scatter(src, dst, send, recv, chips_to, core_to):
+        for j in chips_to:
             pltpu.make_async_remote_copy(
                 src_ref=src.at[j], dst_ref=dst.at[chip], send_sem=send.at[j], recv_sem=recv.at[chip],
-                device_id={"ep": 2 * j + core}, device_id_type=MESH,
+                device_id={"ep": 2 * j + core_to}, device_id_type=MESH,
             ).start()
 
     def transfer(src, dst, send, recv):
@@ -97,7 +97,7 @@
             src_ref=src, dst_ref=dst, send_sem=send, recv_sem=recv, device_id=partner, device_id_type=MESH,
         )
 
-    scatter(picked, slots.at[core], send1, recv1)
+    scatter(picked, slots.at[core], send1, recv1, peers, core)
 
     depth = gate_t.shape[1]
     hidden_size = gate_v.shape[0]
@@ -165,11 +165,11 @@
                 partial = jnp.concatenate([partial, jnp.zeros((chips, piece - size), BF16)], axis=1)
             share[plane, i] = partial
 
-            @pl.when(core != plane)
+            @pl.when(core == plane)
             def _():
                 exchange(plane, i).start()
 
-        @pl.when(core == plane)
+        @pl.when(core != plane)
         def _():
             for i in range(pieces):
                 exchange(plane, i).wait_recv()
@@ -178,10 +178,9 @@
                 summed[:, first : first + piece // LANES, :] = total.reshape(
                     chips, piece // LANES, LANES
                 ).astype(BF16)
-            results[chip] = summed[chip]
-            scatter(summed, results, send2, recv2)
-
-    for j in peers[::-1]:
+            scatter(summed, results, send2, recv2, peers + [chip], plane)
+
+    for j in (peers + [chip])[::-1]:
         transfer(results.at[j], results.at[j], send2.at[j], recv2.at[j]).wait_recv()
 
     mixtures = []
@@ -196,11 +195,12 @@
 
     for j in peers:
         transfer(picked.at[j], picked.at[j], send1.at[j], recv1.at[j]).wait_send()
+    for j in peers + [chip]:
         transfer(summed.at[j], summed.at[j], send2.at[j], recv2.at[j]).wait_send()
     for g in range(half):
         forward(core, g).wait_send()
     for i in range(pieces):
-        exchange(1 - core, i).wait_send()
+        exchange(core, i).wait_send()
 
 
 def shards(tokens, norm_gain, expert_ids, gate_codes, w_gate, w_up, w_down):

time: 50.7 us -> 50 us (0.986)
  Pallas kernels: 50 us -> 49.2 us
    pallas_call x1, Pallas kernels: 50 us -> 49.2 us  [shards(): pl.pallas_call(functools.partial(kernel, side, tiles), out_shape=jax.Shap...]
where the time goes in v7:
time: 50 us; the launch traced here: 49.8 us
  Pallas kernels  49.2 us (98%)
  local copies, waits for them, and re-layouts  0.62 us (1%)
    pallas_call x1, Pallas kernels, shards(): pl.pallas_call(functools.partial(kernel, side, tiles), out_shape=jax.Shap...  49.2 us

profile of v7, /device:TPU:640, one launch (start us, length us, event | category | flops | bytes accessed | tf_op | source)
XLA Modules:
  0.0 49.8 jit_solution(15940595769913504399)
XLA Ops:
  0.0 49.2 %shard_map.73 = bf16[8,2880]{1,0:T(8,128)(2,1)S(1)} custom-call(bf16[8,2880]{1,0:T(8,128)(2,1)} %tokens_hbm.1, f32[2880]{0:T(1024)} %gain_hbm.1, s32[4,8]{1,0:T(4,128)} %bitcast.6, s32[4,8]{1,0:T(4,128)} %bitcast.7, bf16[1,720,2880]{2,1,0:T(8,128)(2,1)} %bitcast.4, bf16[1,720,2880]{2,1,0:T(8,128)(2,1)} %bitcast.5, bf16[1,720,2880]{2,1,0:T(8,128)(2,1)} %down_hbm.1), custom_call_target="tpu_custom_call" | custom-call | tf_op jit(solution)/shard_map/pallas_call | solution.py:218
  49.2 0.6 %copy.9 = bf16[8,2880]{1,0:T(8,128)(2,1)} copy(bf16[8,2880]{1,0:T(8,128)(2,1)S(1)} %shard_map.73) | data formatting | bytes 92160

commit v8 on v7

--- a/solution.py
+++ b/solution.py
@@ -40,6 +40,8 @@
     columns_at = [lax.rem(column + d, side) for d in range(side)]
     offsets.sort(key=lambda o: -(near(o[0]) + near(o[1])))
     peers = [rows_at[dy] + columns_at[dx] for dy, dx in offsets]
+    offsets.sort(key=lambda o: (-near(o[0]), -near(o[1])))
+    peers_back = [rows_at[dy] + columns_at[dx] for dy, dx in offsets]
 
     barrier = pltpu.get_barrier_semaphore()
     for j in peers:
@@ -58,7 +60,7 @@
     for copy in small:
         copy.start()
     weights = [
-        pltpu.make_async_copy(src.at[0], dst, weight_sem.at[i])
+        pltpu.make_async_copy(src.at[0], dst.at[pl.ds(0, src.shape[1])], weight_sem.at[i])
         for i, (src, dst) in enumerate([(gate_hbm, gate_v), (up_hbm, up_v), (down_hbm, down_v)])
     ]
 
@@ -99,8 +101,10 @@
 
     scatter(picked, slots.at[core], send1, recv1, peers, core)
 
+    arrived[chips:, :] = jnp.zeros((arrived.shape[0] - chips, padded), BF16)
     depth = gate_t.shape[1]
     hidden_size = gate_v.shape[0]
+    down_v[hidden_size:, :] = jnp.zeros((depth - hidden_size, width), BF16)
     for i, (src, dst) in enumerate([(gate_v, gate_t), (up_v, up_t)]):
         weights[i].wait()
         dst[:, hidden_size:] = jnp.zeros((dst.shape[0], depth - hidden_size), BF16)
@@ -149,11 +153,11 @@
             for g in groups:
                 forward(plane, g).wait_recv()
 
-        arrived[...] = slots[plane].reshape(chips, padded)
+        arrived[:chips, :] = slots[plane].reshape(chips, padded)
         rows_in = arrived[:, : gate_t.shape[0]]
         gate_out = jnp.dot(rows_in, gate_t[...], preferred_element_type=F32)
         upward = jnp.dot(rows_in, up_t[...], preferred_element_type=F32)
-        hidden = (gate_out / (1.0 + jnp.exp(-gate_out)) * upward).astype(BF16)[:, :hidden_size]
+        hidden = (gate_out / (1.0 + jnp.exp(-gate_out)) * upward).astype(BF16)
         if plane == 1:
             weights[2].wait()
         for i, size in enumerate(sizes):
@@ -162,8 +166,8 @@
                 hidden, down_v[:, low : low + size], preferred_element_type=F32
             ).astype(BF16)
             if size < piece:
-                partial = jnp.concatenate([partial, jnp.zeros((chips, piece - size), BF16)], axis=1)
-            share[plane, i] = partial
+                partial = jnp.concatenate([partial, jnp.zeros((partial.shape[0], piece - size), BF16)], axis=1)
+            share[plane, i] = partial[:chips]
 
             @pl.when(core == plane)
             def _():
@@ -178,9 +182,9 @@
                 summed[:, first : first + piece // LANES, :] = total.reshape(
                     chips, piece // LANES, LANES
                 ).astype(BF16)
-            scatter(summed, results, send2, recv2, peers + [chip], plane)
-
-    for j in (peers + [chip])[::-1]:
+            scatter(summed, results, send2, recv2, peers_back + [chip], plane)
+
+    for j in (peers_back + [chip])[::-1]:
         transfer(results.at[j], results.at[j], send2.at[j], recv2.at[j]).wait_recv()
 
     mixtures = []
@@ -228,12 +232,12 @@
             pltpu.SMEM(gate_codes.shape[::-1], jnp.int32),
             pltpu.VMEM((shard_ff, width), BF16),
             pltpu.VMEM((shard_ff, width), BF16),
-            pltpu.VMEM((shard_ff, width), BF16),
+            pltpu.VMEM((2 * LANES * pl.cdiv(shard_ff, 2 * LANES), width), BF16),
             turned,
             turned,
             blocks,
             pltpu.VMEM((2, chips, tiles, LANES), BF16),
-            pltpu.VMEM((chips, tiles * LANES), BF16),
+            pltpu.VMEM((2 * chips, tiles * LANES), BF16),
             pltpu.VMEM((2,) + shares, BF16),
             pltpu.VMEM(shares, BF16),
             blocks,

time: 50 us -> 48.9 us (0.978)
  Pallas kernels: 49.2 us -> 48.1 us
    pallas_call x1, Pallas kernels: 49.2 us -> 48.1 us  [shards(): pl.pallas_call(functools.partial(kernel, side, tiles), out_shape=jax.Shap...]
where the time goes in v8:
time: 48.9 us; the launch traced here: 48.7 us
  Pallas kernels  48.1 us (98%)
  local copies, waits for them, and re-layouts  0.62 us (1%)
    pallas_call x1, Pallas kernels, shards(): pl.pallas_call(functools.partial(kernel, side, tiles), out_shape=jax.Shap...  48.1 us

profile of v8, /device:TPU:640, one launch (start us, length us, event | category | flops | bytes accessed | tf_op | source)
XLA Modules:
  0.0 48.7 jit_solution(16186008097748728115)
XLA Ops:
  0.0 48.1 %shard_map.73 = bf16[8,2880]{1,0:T(8,128)(2,1)S(1)} custom-call(bf16[8,2880]{1,0:T(8,128)(2,1)} %tokens_hbm.1, f32[2880]{0:T(1024)} %gain_hbm.1, s32[4,8]{1,0:T(4,128)} %bitcast.6, s32[4,8]{1,0:T(4,128)} %bitcast.7, bf16[1,720,2880]{2,1,0:T(8,128)(2,1)} %bitcast.4, bf16[1,720,2880]{2,1,0:T(8,128)(2,1)} %bitcast.5, bf16[1,720,2880]{2,1,0:T(8,128)(2,1)} %down_hbm.1), custom_call_target="tpu_custom_call" | custom-call | tf_op jit(solution)/shard_map/pallas_call | solution.py:222
  48.1 0.6 %copy.9 = bf16[8,2880]{1,0:T(8,128)(2,1)} copy(bf16[8,2880]{1,0:T(8,128)(2,1)S(1)} %shard_map.73) | data formatting | bytes 92160

commit v9 on v8

--- a/solution.py
+++ b/solution.py
@@ -145,8 +145,13 @@
                         arrive()
                 forward(plane, g).start()
 
+    early = lax.axis_index("groups") > 0
+    pl.when(early)(lambda: receive(0))
     for plane in (1, 0):
-        receive(plane)
+        if plane == 1:
+            receive(1)
+        else:
+            pl.when(jnp.logical_not(early))(lambda: receive(0))
 
         @pl.when(core != plane)
         def _():
@@ -184,19 +189,6 @@
                 ).astype(BF16)
             scatter(summed, results, send2, recv2, peers_back + [chip], plane)
 
-    for j in (peers_back + [chip])[::-1]:
-        transfer(results.at[j], results.at[j], send2.at[j], recv2.at[j]).wait_recv()
-
-    mixtures = []
-    for t in range(count):
-        codes = [codes_s[k, t] for k in range(top)]
-        mixture = sum(
-            results[ids_s[k, t]].astype(F32) * codes[k].astype(F32) for k in range(top)
-        )
-        mixtures.append(mixture / jnp.full(mixture.shape, sum(codes).astype(F32)))
-    mixture = jnp.stack(mixtures).reshape(count, padded)[:, :width]
-    out_ref[...] = (tokens_v[...].astype(F32) + mixture).astype(BF16)
-
     for j in peers:
         transfer(picked.at[j], picked.at[j], send1.at[j], recv1.at[j]).wait_send()
     for j in peers + [chip]:
@@ -205,6 +197,19 @@
         forward(core, g).wait_send()
     for i in range(pieces):
         exchange(core, i).wait_send()
+
+    for j in (peers_back + [chip])[::-1]:
+        transfer(results.at[j], results.at[j], send2.at[j], recv2.at[j]).wait_recv()
+
+    mixtures = []
+    for t in range(count):
+        codes = [codes_s[k, t] for k in range(top)]
+        mixture = sum(
+            results[ids_s[k, t]].astype(F32) * codes[k].astype(F32) for k in range(top)
+        )
+        mixtures.append(mixture / jnp.full(mixture.shape, sum(codes).astype(F32)))
+    mixture = jnp.stack(mixtures).reshape(count, padded)[:, :width]
+    out_ref[...] = (tokens_v[...].astype(F32) + mixture).astype(BF16)
 
 
 def shards(tokens, norm_gain, expert_ids, gate_codes, w_gate, w_up, w_down):

time: 48.9 us -> 48.5 us (level)
  no operation moved by 1% of the time
where the time goes in v9:
time: 48.5 us; the launch traced here: 48.4 us
  Pallas kernels  47.7 us (98%)
  local copies, waits for them, and re-layouts  0.62 us (1%)
    pallas_call x1, Pallas kernels, shards(): pl.pallas_call(functools.partial(kernel, side, tiles), out_shape=jax.Shap...  47.7 us

profile of v9, /device:TPU:640, one launch (start us, length us, event | category | flops | bytes accessed | tf_op | source)
XLA Modules:
  0.0 48.4 jit_solution(2146792337436537173)
XLA Ops:
  0.0 47.7 %shard_map.73 = bf16[8,2880]{1,0:T(8,128)(2,1)S(1)} custom-call(bf16[8,2880]{1,0:T(8,128)(2,1)} %tokens_hbm.1, f32[2880]{0:T(1024)} %gain_hbm.1, s32[4,8]{1,0:T(4,128)} %bitcast.6, s32[4,8]{1,0:T(4,128)} %bitcast.7, bf16[1,720,2880]{2,1,0:T(8,128)(2,1)} %bitcast.4, bf16[1,720,2880]{2,1,0:T(8,128)(2,1)} %bitcast.5, bf16[1,720,2880]{2,1,0:T(8,128)(2,1)} %down_hbm.1), custom_call_target="tpu_custom_call" | custom-call | tf_op jit(solution)/shard_map/pallas_call | solution.py:227
  47.7 0.6 %copy.9 = bf16[8,2880]{1,0:T(8,128)(2,1)} copy(bf16[8,2880]{1,0:T(8,128)(2,1)S(1)} %shard_map.73) | data formatting | bytes 92160
